TPU v7x, 32 devices: a whole 2x2x4 slice. The times are simulated.
32 devices in a mesh: fsdp: 4 (over y, x), ctx: 4 (over z), tp: 2 (over core).
Axes of the slice: x: 2, y: 2, z: 4, core: 2. Of those that a mesh axis runs over, the one named last changes fastest.
Arguments:
- tokens: bfloat16 [4, 512, 2560], P('fsdp', 'ctx'), may hold values from -6 to 6
- segment_ids: int32 [4, 512], P('fsdp'), may hold values from 0 to 1, never falling along the last dimension, each value on 1 to 511 neighbouring positions
- w_query: bfloat16 [2560, 2560], P('fsdp', 'tp'), may hold values from -0.125 to 0.125
- w_keyval: bfloat16 [2560, 512], P('fsdp'), may hold values from -0.125 to 0.125
- w_out: bfloat16 [2560, 2560], P('tp', 'fsdp'), may hold values from -1 to 1
- w_gate: bfloat16 [2560, 7680], P('fsdp', 'tp'), may hold values from -0.125 to 0.125
- w_up: bfloat16 [2560, 7680], P('fsdp', 'tp'), may hold values from -0.125 to 0.125
- w_down: bfloat16 [7680, 2560], P('tp', 'fsdp'), may hold values from -0.0625 to 0.0625
- gain_attn: bfloat16 [2560], P('fsdp'), may hold values from 0.5 to 1.5
- gain_ffn: bfloat16 [2560], P('fsdp'), may hold values from 0.5 to 1.5
- cotangent: bfloat16 [4, 512, 2560], P('fsdp', 'ctx'), may hold values from -6 to 6
Outputs:
- out: bfloat16 [4, 512, 2560], P('fsdp', 'ctx')
- grad_tokens: float32 [4, 512, 2560], P('fsdp', 'ctx')
- grad_w_query: float32 [2560, 2560], P('fsdp', 'tp')
- grad_w_keyval: float32 [2560, 512], P('fsdp')
- grad_w_out: float32 [2560, 2560], P('tp', 'fsdp')
- grad_w_gate: float32 [2560, 7680], P('fsdp', 'tp')
- grad_w_up: float32 [2560, 7680], P('fsdp', 'tp')
- grad_w_down: float32 [7680, 2560], P('tp', 'fsdp')
- grad_gain_attn: float32 [2560], P('fsdp')
- grad_gain_ffn: float32 [2560], P('fsdp')
Inputs may be any that keep to these rules, and one draw needn't show every extreme that they name: `segment_ids`: in each packed row the segment numbers never fall and start at 0; every number up to 1 is used; a segment has 1 to 511 tokens.
All inputs are finite; a program needn't handle non-finite values.
Results may differ from a plain program's by a relative error of at most 0.023.
Values may be sent and summed in bfloat16 or wider, within the bound.
A program may use at most 384 MiB of HBM per device.

v0:
```python
import jax
import jax.numpy as jnp
from jax import lax
from jax.sharding import PartitionSpec as P

HD = 256


negative = -1e30


def rms_scale(value, gain):
    return value * lax.rsqrt(jnp.mean(value * value, axis=-1, keepdims=True) + 1e-06) * gain


def rotate(value, cosine, sine):
    quarter = value.shape[-1] // 4
    first = value[..., :quarter]
    second = value[..., quarter : 2 * quarter]
    rest = value[..., 2 * quarter :]
    return jnp.concatenate(
        [first * cosine - second * sine, second * cosine + first * sine, rest], axis=-1
    )


def unrotate(value, cosine, sine):
    quarter = value.shape[-1] // 4
    first = value[..., :quarter]
    second = value[..., quarter : 2 * quarter]
    rest = value[..., 2 * quarter :]
    return jnp.concatenate(
        [first * cosine + second * sine, second * cosine - first * sine, rest], axis=-1
    )


def matmul(left, right):
    return jnp.dot(left, right, preferred_element_type=jnp.float32)


def times_transposed(left, right):
    return lax.dot_general(
        left, right, (((1,), (1,)), ((), ())), preferred_element_type=jnp.float32
    )


def transposed_times(left, right):
    return lax.dot_general(
        left, right, (((0,), (0,)), ((), ())), preferred_element_type=jnp.float32
    )


def geglu(gate_in, up_in):
    return jax.nn.gelu(gate_in, approximate=True) * up_in


def per_device(
    tokens,
    segment_ids,
    w_query,
    w_keyval,
    w_out,
    w_gate,
    w_up,
    w_down,
    gain_attn,
    gain_ffn,
    cotangent,
):
    rows_dev = tokens.shape[1]
    heads_dev = w_query.shape[1] // HD
    scale = HD ** (-0.5)
    inputs = tokens[0].astype(jnp.float32)
    gathered = (
        lax.all_gather(w_query, "fsdp", axis=0, tiled=True),
        lax.all_gather(w_keyval, "fsdp", axis=0, tiled=True),
        lax.all_gather(w_out, "fsdp", axis=1, tiled=True),
        lax.all_gather(w_gate, "fsdp", axis=0, tiled=True),
        lax.all_gather(w_up, "fsdp", axis=0, tiled=True),
        lax.all_gather(w_down, "fsdp", axis=1, tiled=True),
        lax.all_gather(gain_attn, "fsdp", axis=0, tiled=True),
        lax.all_gather(gain_ffn, "fsdp", axis=0, tiled=True),
    )
    query_full, keyval_full, out_full, gate_full, up_full, down_full, gain_one, gain_two = gathered
    gain_one = gain_one.astype(jnp.float32)
    gain_two = gain_two.astype(jnp.float32)
    group = segment_ids.shape[1]
    segment_row = segment_ids[0]
    index_all = jnp.arange(group, dtype=jnp.int32)
    change = jnp.concatenate([jnp.ones((1,), dtype=bool), segment_row[1:] != segment_row[:-1]])
    starts = lax.cummax(jnp.where(change, index_all, jnp.zeros_like(index_all)), axis=0)
    position_all = index_all - starts
    offset = lax.axis_index("ctx") * rows_dev
    local_position = lax.dynamic_slice_in_dim(position_all, offset, rows_dev, 0).astype(jnp.float32)
    local_segment = lax.dynamic_slice_in_dim(segment_row, offset, rows_dev, 0)
    local_index = offset + jnp.arange(rows_dev, dtype=jnp.int32)
    freqs = 10000.0 ** (-(jnp.arange(HD // 4, dtype=jnp.float32) * 2.0 / (HD // 2)))
    angle = local_position[:, None] * freqs[None, :]
    cosine = jnp.cos(angle)
    sine = jnp.sin(angle)
    normed_attn = rms_scale(inputs, gain_one).astype(jnp.bfloat16)
    query = matmul(normed_attn, query_full).reshape(rows_dev, heads_dev, HD)
    keyval = matmul(normed_attn, keyval_full)
    query_rot = rotate(query, cosine[:, None, :], sine[:, None, :])
    query_rows = query_rot.reshape(rows_dev * heads_dev, HD).astype(jnp.bfloat16)
    key_local = rotate(keyval[:, :HD], cosine, sine).astype(jnp.bfloat16)
    value_local = keyval[:, HD:].astype(jnp.bfloat16)
    key_all, value_all = (
        lax.all_gather(key_local, "ctx", axis=0, tiled=True),
        lax.all_gather(value_local, "ctx", axis=0, tiled=True),
    )
    row_count = rows_dev * heads_dev
    row_index = jnp.repeat(local_index, heads_dev)
    row_segment = jnp.repeat(local_segment, heads_dev)
    block = min(512, group)
    block_count = group // block
    numbers = jnp.arange(block_count, dtype=jnp.int32)

    def block_scores(number):
        begin = number * block
        key_block = lax.dynamic_slice_in_dim(key_all, begin, block, 0)
        value_block = lax.dynamic_slice_in_dim(value_all, begin, block, 0)
        segment_block = lax.dynamic_slice_in_dim(segment_row, begin, block, 0)
        index_block = begin + jnp.arange(block, dtype=jnp.int32)
        scores = times_transposed(query_rows, key_block) * scale
        mask = (row_segment[:, None] == segment_block[None, :]) & (
            index_block[None, :] <= row_index[:, None]
        )
        return (jnp.where(mask, scores, negative), mask, key_block, value_block)

    def stats_step(carry, number):
        peak, total = carry
        scores, mask, key_block, value_block = block_scores(number)
        new_peak = jnp.maximum(peak, jnp.max(scores, axis=1))
        terms = jnp.where(mask, jnp.exp(scores - new_peak[:, None]), 0.0)
        return ((new_peak, total * jnp.exp(peak - new_peak) + jnp.sum(terms, axis=1)), None)

    init_stats = (
        jnp.full((row_count,), negative, jnp.float32),
        jnp.zeros((row_count,), jnp.float32),
    )
    (peak, total), unused = lax.scan(stats_step, init_stats, numbers)
    log_total = peak + jnp.log(total)

    def value_step(carry, number):
        main_sum, rest_sum = carry
        scores, mask, key_block, value_block = block_scores(number)
        probs = jnp.where(mask, jnp.exp(scores - log_total[:, None]), 0.0)
        probs_low = probs.astype(jnp.bfloat16)
        probs_rest = (probs - probs_low.astype(jnp.float32)).astype(jnp.bfloat16)
        return (
            (main_sum + matmul(probs_low, value_block), rest_sum + matmul(probs_rest, value_block)),
            None,
        )

    zero_rows = jnp.zeros((row_count, HD), jnp.float32)
    (main_sum, rest_sum), unused = lax.scan(value_step, (zero_rows, zero_rows), numbers)
    attended_exact = main_sum + rest_sum
    attended = main_sum.reshape(rows_dev, heads_dev * HD).astype(jnp.bfloat16)
    branch = lax.psum(matmul(attended, out_full).astype(jnp.bfloat16), "tp").astype(jnp.float32)
    hidden_state = inputs + branch
    normed_ffn = rms_scale(hidden_state, gain_two).astype(jnp.bfloat16)
    gate = matmul(normed_ffn, gate_full)
    upward = matmul(normed_ffn, up_full)
    hidden = geglu(gate, upward).astype(jnp.bfloat16)
    feed = lax.psum(matmul(hidden, down_full).astype(jnp.bfloat16), "tp").astype(jnp.float32)
    output = (hidden_state + feed).astype(jnp.bfloat16)
    again = (
        lax.all_gather(w_query, "fsdp", axis=0, tiled=True),
        lax.all_gather(w_keyval, "fsdp", axis=0, tiled=True),
        lax.all_gather(w_out, "fsdp", axis=1, tiled=True),
        lax.all_gather(w_gate, "fsdp", axis=0, tiled=True),
        lax.all_gather(w_up, "fsdp", axis=0, tiled=True),
        lax.all_gather(w_down, "fsdp", axis=1, tiled=True),
    )
    query_back, keyval_back, out_back, gate_back, up_back, down_back = again
    incoming = cotangent[0]
    d_hidden = times_transposed(incoming, down_back)
    grad_down = transposed_times(hidden, incoming)
    unused_value, geglu_pull = jax.vjp(geglu, gate, upward)
    d_gate, d_up = geglu_pull(d_hidden)
    d_gate = d_gate.astype(jnp.bfloat16)
    d_up = d_up.astype(jnp.bfloat16)
    grad_gate = transposed_times(normed_ffn, d_gate)
    grad_up = transposed_times(normed_ffn, d_up)
    d_normed_ffn = lax.psum(
        (times_transposed(d_gate, gate_back) + times_transposed(d_up, up_back)).astype(
            jnp.bfloat16
        ),
        "tp",
    ).astype(jnp.float32)
    unused_value, norm_pull = jax.vjp(rms_scale, hidden_state, gain_two)
    d_state_norm, grad_gain_two = norm_pull(d_normed_ffn)
    d_state = incoming.astype(jnp.float32) + d_state_norm
    d_branch = d_state.astype(jnp.bfloat16)
    grad_out = transposed_times(attended, d_branch)
    d_attended = times_transposed(d_branch, out_back).reshape(row_count, HD).astype(jnp.bfloat16)
    delta = jnp.sum(d_attended.astype(jnp.float32) * attended_exact, axis=1)

    def grad_step(d_rows, number):
        scores, mask, key_block, value_block = block_scores(number)
        probs = jnp.where(mask, jnp.exp(scores - log_total[:, None]), 0.0)
        probs_low = probs.astype(jnp.bfloat16)
        d_probs = times_transposed(d_attended, value_block)
        d_scores = (probs * (d_probs - delta[:, None])).astype(jnp.bfloat16)
        new_rows = d_rows + matmul(d_scores, key_block) * scale
        d_key_block = transposed_times(d_scores, query_rows) * scale
        d_value_block = transposed_times(probs_low, d_attended)
        return (new_rows, (d_key_block, d_value_block))

    d_rows, (d_key_blocks, d_value_blocks) = lax.scan(grad_step, zero_rows, numbers)
    d_key_all = d_key_blocks.reshape(group, HD)
    d_value_all = d_value_blocks.reshape(group, HD)
    d_key_mine, d_value_mine = (
        lax.psum_scatter(
            d_key_all.astype(jnp.bfloat16), "ctx", scatter_dimension=0, tiled=True
        ).astype(jnp.float32),
        lax.psum_scatter(
            d_value_all.astype(jnp.bfloat16), "ctx", scatter_dimension=0, tiled=True
        ).astype(jnp.float32),
    )
    d_query = unrotate(
        d_rows.reshape(rows_dev, heads_dev, HD), cosine[:, None, :], sine[:, None, :]
    )
    d_query = d_query.reshape(rows_dev, heads_dev * HD).astype(jnp.bfloat16)
    d_normed_query = times_transposed(d_query, query_back)
    d_normed_query, d_key_mine, d_value_mine = (
        lax.psum(d_normed_query.astype(jnp.bfloat16), "tp").astype(jnp.float32),
        lax.psum(d_key_mine.astype(jnp.bfloat16), "tp").astype(jnp.float32),
        lax.psum(d_value_mine.astype(jnp.bfloat16), "tp").astype(jnp.float32),
    )
    d_keyval = jnp.concatenate([unrotate(d_key_mine, cosine, sine), d_value_mine], axis=1).astype(
        jnp.bfloat16
    )
    d_normed_attn = d_normed_query + times_transposed(d_keyval, keyval_back)
    grad_query = transposed_times(normed_attn, d_query)
    grad_keyval = transposed_times(normed_attn, d_keyval)
    unused_value, norm_pull_one = jax.vjp(rms_scale, inputs, gain_one)
    d_input_norm, grad_gain_one = norm_pull_one(d_normed_attn)
    grad_inputs = d_state + d_input_norm
    shards = (
        lax.psum_scatter(
            grad_query.astype(jnp.bfloat16), "fsdp", scatter_dimension=0, tiled=True
        ).astype(jnp.float32),
        lax.psum_scatter(
            grad_keyval.astype(jnp.bfloat16), "fsdp", scatter_dimension=0, tiled=True
        ).astype(jnp.float32),
        lax.psum_scatter(
            grad_out.astype(jnp.bfloat16), "fsdp", scatter_dimension=1, tiled=True
        ).astype(jnp.float32),
        lax.psum_scatter(
            grad_gate.astype(jnp.bfloat16), "fsdp", scatter_dimension=0, tiled=True
        ).astype(jnp.float32),
        lax.psum_scatter(
            grad_up.astype(jnp.bfloat16), "fsdp", scatter_dimension=0, tiled=True
        ).astype(jnp.float32),
        lax.psum_scatter(
            grad_down.astype(jnp.bfloat16), "fsdp", scatter_dimension=1, tiled=True
        ).astype(jnp.float32),
        lax.psum_scatter(
            grad_gain_one.astype(jnp.bfloat16), "fsdp", scatter_dimension=0, tiled=True
        ).astype(jnp.float32),
        lax.psum_scatter(
            grad_gain_two.astype(jnp.bfloat16), "fsdp", scatter_dimension=0, tiled=True
        ).astype(jnp.float32),
    )
    shards = (
        lax.psum(shards[0].astype(jnp.bfloat16), "ctx").astype(jnp.float32),
        lax.psum(shards[1].astype(jnp.bfloat16), "ctx").astype(jnp.float32),
        lax.psum(shards[2].astype(jnp.bfloat16), "ctx").astype(jnp.float32),
        lax.psum(shards[3].astype(jnp.bfloat16), "ctx").astype(jnp.float32),
        lax.psum(shards[4].astype(jnp.bfloat16), "ctx").astype(jnp.float32),
        lax.psum(shards[5].astype(jnp.bfloat16), "ctx").astype(jnp.float32),
        lax.psum(shards[6].astype(jnp.bfloat16), "ctx").astype(jnp.float32),
        lax.psum(shards[7].astype(jnp.bfloat16), "ctx").astype(jnp.float32),
    )
    return (
        output[None],
        grad_inputs[None],
        shards[0],
        shards[1],
        shards[2],
        shards[3],
        shards[4],
        shards[5],
        shards[6],
        shards[7],
    )


def solution(mesh):
    in_specs = (
        P("fsdp", "ctx", None),
        P("fsdp", None),
        P("fsdp", "tp"),
        P("fsdp", None),
        P("tp", "fsdp"),
        P("fsdp", "tp"),
        P("fsdp", "tp"),
        P("tp", "fsdp"),
        P("fsdp"),
        P("fsdp"),
        P("fsdp", "ctx", None),
    )
    out_specs = (
        P("fsdp", "ctx", None),
        P("fsdp", "ctx", None),
        P("fsdp", "tp"),
        P("fsdp", None),
        P("tp", "fsdp"),
        P("fsdp", "tp"),
        P("fsdp", "tp"),
        P("tp", "fsdp"),
        P("fsdp"),
        P("fsdp"),
    )
    return jax.shard_map(
        per_device, mesh=mesh, in_specs=in_specs, out_specs=out_specs, check_vma=False
    )
```

profile of v0, /device:TPU:0, one launch (start us, length us, event | category | flops | bytes accessed | tf_op | source)
XLA Modules:
  0.0 2314.9 jit_solution(12491903185718337529)
XLA Ops:
  9.5 9.7 all-gather
  21.0 31.1 %all-gather.11.cloned.1.call-done = bf16[2560,512]{1,0:T(8,128)(2,1)} async-done(((bf16[640,512]{1,0:T(8,128)(2,1)}), bf16[2560,512]{1,0:T(8,128)(2,1)}) %all-gather.11.cloned.1.call-update) | async-done | bytes 2621456 | tf_op jit(solution)/shard_map/all_gather | solution.py:75
  54.4 13.8 all_gather.40
  68.7 14.6 all_gather.39
  83.4 42.8 %all-gather.9.cloned.1.call-done = bf16[2560,1280]{1,0:T(8,128)(2,1)} async-done(((bf16[640,1280]{1,0:T(8,128)(2,1)}), bf16[2560,1280]{1,0:T(8,128)(2,1)}) %all-gather.9.cloned.1.call-update) | async-done | bytes 6553616 | tf_op jit(solution)/shard_map/all_gather | solution.py:74
  126.2 9.6 copy.43
  135.8 5.9 fusion.39
  145.5 54.7 %all-gather.13.cloned.1.call-done = bf16[1280,2560]{1,0:T(8,128)(2,1)} async-done(((bf16[1280,640]{1,0:T(8,128)(2,1)}), bf16[1280,2560]{1,0:T(8,128)(2,1)}) %all-gather.13.cloned.1.call-update) | async-done | bytes 6553616 | tf_op jit(solution)/shard_map/all_gather | solution.py:76
  200.3 4.7 convolution_convert_fusion.8
  207.0 8.4 all-gather.1
  215.5 8.5 all-reduce.11.cloned.1.call-done
  225.7 183.5 %all-gather.15.cloned.1.call-done = bf16[2560,3840]{1,0:T(8,128)(2,1)} async-done(((bf16[640,3840]{1,0:T(8,128)(2,1)}), bf16[2560,3840]{1,0:T(8,128)(2,1)}) %all-gather.15.cloned.1.call-update) | async-done | bytes 19660816 | tf_op jit(solution)/shard_map/all_gather | solution.py:77
  409.2 10.7 fusion.79
  419.9 173.3 %all-gather.17.cloned.1.call-done = bf16[2560,3840]{1,0:T(8,128)(2,1)} async-done(((bf16[640,3840]{1,0:T(8,128)(2,1)}), bf16[2560,3840]{1,0:T(8,128)(2,1)}) %all-gather.17.cloned.1.call-update) | async-done | bytes 19660816 | tf_op jit(solution)/shard_map/all_gather | solution.py:78
  593.2 10.7 fusion.80
  603.9 173.5 %all-gather.19.cloned.1.call-done = bf16[3840,2560]{1,0:T(8,128)(2,1)} async-done(((bf16[3840,640]{1,0:T(8,128)(2,1)}), bf16[3840,2560]{1,0:T(8,128)(2,1)}) %all-gather.19.cloned.1.call-update) | async-done | bytes 19660816 | tf_op jit(solution)/shard_map/all_gather | solution.py:79
  777.4 13.0 multiply_convert_fusion
  790.4 14.2 fusion.81
  804.6 11.4 fusion
  816.3 10.4 convolution_convert_fusion.6
  826.7 8.4 all-reduce.13.cloned.1.call-done
  838.1 5.9 convolution_convert_fusion.9
  866.9 6.1 convolution_convert_fusion.7
  873.0 6.2 reduce-scatter.15.cloned.1.call-done
  879.2 21.0 reduce-scatter.13.cloned.1.call-done
  900.4 6.1 convolution_convert_fusion.3
  906.5 9.5 copy.53
  916.1 10.5 convolution_convert_fusion
  926.6 24.2 %copy.55 = bf16[3840,2560]{0,1:T(8,128)(2,1)} copy(bf16[3840,2560]{1,0:T(8,128)(2,1)} %convolution_convert_fusion) | data formatting | bytes 39321600
  957.1 4.8 convolution_convert_fusion.4
  963.1 9.5 convolution_convert_fusion.2
  973.8 9.9 convolution_convert_fusion.1
  983.8 14.9 reduce-scatter.25.cloned.1.call-done
  998.7 3.5 copy.54
  1002.3 176.7 %reduce-scatter.27.cloned.1.call-done = bf16[640,3840]{1,0:T(8,128)(2,1)} async-done(((bf16[2560,3840]{1,0:T(8,128)(2,1)}), bf16[640,3840]{1,0:T(8,128)(2,1)}) %reduce-scatter.27.cloned.1.call-update) | async-done | bytes 4915216
  1179.0 7.7 copy.56
  1186.7 35.3 %reduce-scatter.19.cloned.1.call-done = bf16[640,512]{1,0:T(8,128)(2,1)} async-done(((bf16[2560,512]{1,0:T(8,128)(2,1)}), bf16[640,512]{1,0:T(8,128)(2,1)}) %reduce-scatter.19.cloned.1.call-update) | async-done | bytes 655376 | tf_op jit(solution)/shard_map/reduce_scatter | solution.py:244
  1222.0 75.7 %reduce-scatter.17.cloned.1.call-done = bf16[640,1280]{1,0:T(8,128)(2,1)} async-done(((bf16[2560,1280]{1,0:T(8,128)(2,1)}), bf16[640,1280]{1,0:T(8,128)(2,1)}) %reduce-scatter.17.cloned.1.call-update) | async-done | bytes 1638416 | tf_op jit(solution)/shard_map/reduce_scatter | solution.py:241
  1297.7 180.1 %reduce-scatter.21.cloned.1.call-done = bf16[640,3840]{1,0:T(8,128)(2,1)} async-done(((bf16[2560,3840]{1,0:T(8,128)(2,1)}), bf16[640,3840]{1,0:T(8,128)(2,1)}) %reduce-scatter.21.cloned.1.call-update) | async-done | bytes 4915216 | tf_op jit(solution)/shard_map/reduce_scatter | solution.py:250
  1477.9 180.1 %reduce-scatter.23.cloned.1.call-done = bf16[640,3840]{1,0:T(8,128)(2,1)} async-done(((bf16[2560,3840]{1,0:T(8,128)(2,1)}), bf16[640,3840]{1,0:T(8,128)(2,1)}) %reduce-scatter.23.cloned.1.call-update) | async-done | bytes 4915216 | tf_op jit(solution)/shard_map/reduce_scatter | solution.py:253
  1659.9 4.2 fusion.21
  1664.1 15.0 all-reduce.4
  1679.3 12.3 all-reduce.2
  1692.8 3.5 fusion.30
  1696.3 588.8 %all-reduce.15.cloned.1.call-done = (bf16[640,1280]{1,0:T(8,128)(2,1)}, bf16[640,512]{1,0:T(8,128)(2,1)}, bf16[1280,640]{1,0:T(8,128)(2,1)}, bf16[640,3840]{1,0:...) async-done(((bf16[640,1280]{1,0:T(8,128)(2,1)}, bf16[640,512]{1,0:T(8,128)(2,1)}, bf16[1280,640]{1,0:T(8,128)(2,1)}, bf16[640,3840]{1,0:T(8,128)(2,1)}, ...) | async-done | bytes 18677776 | tf_op jit(solution)/shard_map/psum | solution.py:267
  2293.6 4.9 convert_element_type.250
  2298.5 4.6 convert_element_type.252
  2303.1 4.5 convert_element_type.254
  (229 shorter events, 60.2 us)
Async XLA Ops:
  7.2 44.9 %all-gather.11.cloned.1.call-start = ((), (), s32[]{:S(2)}) async-start(), calls=%async_computation.9 | async-start | bytes 3276800 | tf_op jit(solution)/shard_map/all_gather | solution.py:75
  7.9 11.3 copy-start.31
  7.9 118.2 %all-gather.9.cloned.1.call-start = ((), (), s32[]{:S(2)}) async-start(), calls=%async_computation.8 | async-start | bytes 8192000 | tf_op jit(solution)/shard_map/all_gather | solution.py:74
  8.7 12.1 copy-start
  8.7 191.6 %all-gather.13.cloned.1.call-start = ((), (), s32[]{:S(2)}) async-start(), calls=%async_computation.10 | async-start | bytes 8192000 | tf_op jit(solution)/shard_map/all_gather | solution.py:76
  9.4 214.5 %all-reduce.11.cloned.1.call-start = ((), (), s32[]{:S(2)}) async-start(), calls=%async_computation.11 | async-start | bytes 1310720 | tf_op jit(solution)/shard_map/psum | solution.py:159
  20.1 123.5 %copy-start.33 = (s32[640]{0:T(1024)}, s32[640]{0:T(1024)S(1)}, u32[]{:S(2)}) copy-start(s32[640]{0:T(1024)S(1)} %le.51) | copy-start | bytes 7684
  20.4 123.2 %copy-start.35 = (s32[640]{0:T(1024)}, s32[640]{0:T(1024)S(1)}, u32[]{:S(2)}) copy-start(s32[640]{0:T(1024)S(1)} %eq.52) | copy-start | bytes 7684
  20.5 47.8 %copy-start.42 = (f32[64]{0:T(128)}, f32[64]{0:T(128)S(1)}, u32[]{:S(2)}) copy-start(f32[64]{0:T(128)S(1)} %negate_power_fusion) | copy-start | bytes 772
  20.7 47.5 %copy-start.44 = (f32[128]{0:T(128)}, f32[128]{0:T(128)S(1)}, u32[]{:S(2)}) copy-start(f32[128]{0:T(128)S(1)} %dynamic-slice_convert_fusion) | copy-start | bytes 1540
  21.0 33.4 %copy-start.52 = (f32[128]{0:T(128)}, f32[128]{0:T(128)S(1)}, u32[]{:S(2)}) copy-start(f32[128]{0:T(128)S(1)} %fusion.24) | copy-start | bytes 1540
  68.3 75.4 %copy-start.27 = (bf16[512,256]{1,0:T(8,128)(2,1)}, bf16[512,256]{1,0:T(8,128)(2,1)S(1)}, u32[]{:S(2)}) copy-start(bf16[512,256]{1,0:T(8,128)(2,1)S(1)} %all_gather.40) | copy-start | bytes 786436
  68.6 73.2 %copy-start.18 = (f32[128,64]{1,0:T(8,128)}, f32[128,64]{1,0:T(8,128)S(1)}, u32[]{:S(2)}) copy-start(f32[128,64]{1,0:T(8,128)S(1)} %get-tuple-element.136) | copy-start | bytes 98308
  68.6 73.2 %copy-start.20 = (f32[128,64]{1,0:T(8,128)}, f32[128,64]{1,0:T(8,128)S(1)}, u32[]{:S(2)}) copy-start(f32[128,64]{1,0:T(8,128)S(1)} %get-tuple-element.137) | copy-start | bytes 98308
  205.0 204.2 %all-gather.15.cloned.1.call-start = ((), (), s32[]{:S(2)}) async-start(), calls=%async_computation.12 | async-start | bytes 24576000 | tf_op jit(solution)/shard_map/all_gather | solution.py:77
  205.6 387.6 %all-gather.17.cloned.1.call-start = ((), (), s32[]{:S(2)}) async-start(), calls=%async_computation.13 | async-start | bytes 24576000 | tf_op jit(solution)/shard_map/all_gather | solution.py:78
  206.2 571.2 %all-gather.19.cloned.1.call-start = ((), (), s32[]{:S(2)}) async-start(), calls=%async_computation.14 | async-start | bytes 24576000 | tf_op jit(solution)/shard_map/all_gather | solution.py:79
  206.9 628.1 %all-reduce.13.cloned.1.call-start = ((), (), s32[]{:S(2)}) async-start(), calls=%async_computation.15 | async-start | bytes 1310720 | tf_op jit(solution)/shard_map/psum | solution.py:185
  215.5 10.2 copy-start.24
  225.4 194.5 %copy-start.50 = (f32[128]{0:T(128)}, f32[128]{0:T(128)S(1)}, u32[]{:S(2)}) copy-start(f32[128]{0:T(128)S(1)} %multiply_reduce_fusion) | copy-start | bytes 1540
  225.4 194.4 %copy-start.37 = (f32[128]{0:T(128)}, f32[128]{0:T(128)S(1)}, u32[]{:S(2)}) copy-start(f32[128]{0:T(128)S(1)} %fusion.66) | copy-start | bytes 1540
  816.1 63.1 %reduce-scatter.15.cloned.1.call-start = ((), (), s32[]{:S(2)}) async-start(), calls=%async_computation.17 | async-start | bytes 327680 | tf_op jit(solution)/shard_map/reduce_scatter | solution.py:217
  835.0 3.0 copy-start.38
  857.8 3.4 copy-start.19
  857.8 42.3 %reduce-scatter.13.cloned.1.call-start = ((), (), s32[]{:S(2)}) async-start(), calls=%async_computation.16 | async-start | bytes 327680 | tf_op jit(solution)/shard_map/reduce_scatter | solution.py:214
  857.8 3.3 copy-start.21
  863.1 87.8 %all-reduce.17.cloned.1.call-start = ((), (), s32[]{:S(2)}) async-start(), calls=%async_computation.25 | async-start | bytes 2883584 | tf_op jit(solution)/shard_map/psum | solution.py:165
  873.0 27.4 %copy-start.26 = (f32[2560]{0:T(1024)S(1)}, f32[2560]{0:T(1024)}, u32[]{:S(2)}) copy-start(f32[2560]{0:T(1024)} %copy-done.24) | copy-start | bytes 30724
  873.0 27.4 %copy-start.39 = (f32[128]{0:T(128)S(1)}, f32[128]{0:T(128)}, u32[]{:S(2)}) copy-start(f32[128]{0:T(128)} %copy-done.37) | copy-start | bytes 1540
  873.0 27.5 %copy-start.47 = (f32[128]{0:T(128)S(1)}, f32[128]{0:T(128)}, u32[]{:S(2)}) copy-start(f32[128]{0:T(128)} %copy-done.46) | copy-start | bytes 1540
  900.1 98.6 %reduce-scatter.25.cloned.1.call-start = ((), (), s32[]{:S(2)}) async-start(), calls=%async_computation.22 | async-start | bytes 8192000
  916.0 263.0 %reduce-scatter.27.cloned.1.call-start = ((), (), s32[]{:S(2)}) async-start(), calls=%async_computation.23 | async-start | bytes 24576000
  950.8 271.2 %reduce-scatter.19.cloned.1.call-start = ((), (), s32[]{:S(2)}) async-start(), calls=%async_computation.19 | async-start | bytes 3276800 | tf_op jit(solution)/shard_map/reduce_scatter | solution.py:244
  956.2 341.5 %reduce-scatter.17.cloned.1.call-start = ((), (), s32[]{:S(2)}) async-start(), calls=%async_computation.18 | async-start | bytes 8192000 | tf_op jit(solution)/shard_map/reduce_scatter | solution.py:241
  961.9 515.9 %reduce-scatter.21.cloned.1.call-start = ((), (), s32[]{:S(2)}) async-start(), calls=%async_computation.20 | async-start | bytes 24576000 | tf_op jit(solution)/shard_map/reduce_scatter | solution.py:250
  972.6 685.3 %reduce-scatter.23.cloned.1.call-start = ((), (), s32[]{:S(2)}) async-start(), calls=%async_computation.21 | async-start | bytes 24576000 | tf_op jit(solution)/shard_map/reduce_scatter | solution.py:253
  983.8 1301.4 %all-reduce.15.cloned.1.call-start = ((), (), s32[]{:S(2)}) async-start(), calls=%async_computation.24 | async-start | bytes 37355520 | tf_op jit(solution)/shard_map/psum | solution.py:267
  1659.9 4.3 copy-start.30
  1659.9 32.9 %copy-start.53 = (f32[128]{0:T(128)S(1)}, f32[128]{0:T(128)}, u32[]{:S(2)}) copy-start(f32[128]{0:T(128)} %copy-done.52) | copy-start | bytes 1540
  1659.9 32.9 %copy-start.4 = (bf16[128,2560]{1,0:T(8,128)(2,1)S(1)}, bf16[128,2560]{1,0:T(8,128)(2,1)}, u32[]{:S(2)}) copy-start(bf16[128,2560]{1,0:T(8,128)(2,1)} %all-reduce.13.cloned.1.call-done) | copy-start | bytes 1966084
  1659.9 32.9 %copy-start.6 = (bf16[1,128,2560]{2,1,0:T(8,128)(2,1)S(1)}, bf16[1,128,2560]{2,1,0:T(8,128)(2,1)}, u32[]{:S(2)}) copy-start(bf16[1,128,2560]{2,1,0:T(8,128)(2,1)} %param.21) | copy-start | bytes 1966084
  1659.9 32.9 %copy-start.14 = (bf16[128,2560]{1,0:T(8,128)(2,1)S(1)}, bf16[128,2560]{1,0:T(8,128)(2,1)}, u32[]{:S(2)}) copy-start(bf16[128,2560]{1,0:T(8,128)(2,1)} %get-tuple-element.104) | copy-start | bytes 1966084
  2285.2 3.5 copy-start.17
  2289.9 3.7 copy-start.7
  2290.5 7.9 slice-start.2
  2293.6 4.9 slice-start.3
  2293.6 9.5 slice-start
  2298.5 4.6 slice-start.1
  (29 other events, 55.4 us)
Sparse Core Ops, SparseCore 0:
  9.8 42.2 all-gather.10
  53.9 72.1 all-gather.8
  128.0 72.1 all-gather.12
  205.1 18.7 all-reduce.10
  225.7 183.4 all-gather.14
  410.9 182.2 all-gather.16
  595.1 182.2 all-gather.18
  816.2 18.7 all-reduce.12
  857.9 21.2 reduce-scatter.14
  881.8 18.2 reduce-scatter.12
  903.2 18.5 all-reduce.16
  925.3 73.4 reduce-scatter.24
  1001.9 177.0 reduce-scatter.26
  1182.4 39.5 reduce-scatter.18
  1225.5 72.1 reduce-scatter.16
  1300.7 177.1 reduce-scatter.20
  1480.8 177.0 reduce-scatter.22
  1661.7 623.4 all-reduce.14
where the time goes:
time: 2320 us; the launch traced here: 2310 us
  waiting for transfers between devices  1960 us (84%)
  matrix products  153 us (7%)
  local copies, waits for them, and re-layouts  75.8 us (3%)
  blocking collectives  73.9 us (3%)
  other arithmetic  35.5 us (2%)
    psum x1, waiting for transfers between devices, per_device(): lax.psum(shards[0].astype(jnp.bfloat16), 'ctx').astype(jnp.float32)  589 us
    unnamed x20, waiting for transfers between devices  196 us
    all_gather x1, waiting for transfers between devices, per_device(): lax.all_gather(w_gate, 'fsdp', axis=0, tiled=True)  183 us
    reduce_scatter x1, waiting for transfers between devices, per_device(): lax.psum_scatter(grad_gate.astype(jnp.bfloat16), 'fsdp', scatter_dimensio...  180 us
    reduce_scatter x1, waiting for transfers between devices, per_device(): lax.psum_scatter(grad_up.astype(jnp.bfloat16), 'fsdp', scatter_dimension=...  180 us
    all_gather x1, waiting for transfers between devices, per_device(): lax.all_gather(w_down, 'fsdp', axis=1, tiled=True)  174 us
    all_gather x1, waiting for transfers between devices, per_device(): lax.all_gather(w_up, 'fsdp', axis=0, tiled=True)  173 us
    reduce_scatter x1, waiting for transfers between devices, per_device(): lax.psum_scatter(grad_query.astype(jnp.bfloat16), 'fsdp', scatter_dimensi...  75.7 us
  transfers between devices with their start and end apart: 18, of which 17 were waited for; matrix products, arithmetic and copies ran while one was open for 7% of the time, Pallas kernels for 0%

commit v1 on v0

v1 whole, which is shorter than its diff:
```python
import jax
import jax.numpy as jnp
from jax import lax
from jax.sharding import PartitionSpec as P

HD = 256
NEGATIVE = -1e30
BF = jnp.bfloat16
F32 = jnp.float32


def rms_scale(value, gain):
    return value * lax.rsqrt(jnp.mean(value * value, axis=-1, keepdims=True) + 1e-06) * gain


def rotate(value, cosine, sine):
    quarter = value.shape[-1] // 4
    first = value[..., :quarter]
    second = value[..., quarter : 2 * quarter]
    rest = value[..., 2 * quarter :]
    return jnp.concatenate(
        [first * cosine - second * sine, second * cosine + first * sine, rest], axis=-1
    )


def unrotate(value, cosine, sine):
    return rotate(value, cosine, -sine)


def matmul(left, right):
    return jnp.dot(left, right, preferred_element_type=F32)


def times_transposed(left, right):
    return lax.dot_general(left, right, (((1,), (1,)), ((), ())), preferred_element_type=F32)


def transposed_times(left, right):
    return lax.dot_general(left, right, (((0,), (0,)), ((), ())), preferred_element_type=F32)


def geglu(gate_in, up_in):
    return jax.nn.gelu(gate_in, approximate=True) * up_in


def swap(value, axis, size, k):
    return lax.ppermute(value, axis, [(i, i ^ k) for i in range(size)])


def per_device(
    sizes,
    tokens,
    segment_ids,
    w_query,
    w_keyval,
    w_out,
    w_gate,
    w_up,
    w_down,
    gain_attn,
    gain_ffn,
    cotangent,
):
    nf, nc, nt = sizes
    fi, ci, ti = lax.axis_index("fsdp"), lax.axis_index("ctx"), lax.axis_index("tp")
    rows = tokens.shape[1]
    depth = tokens.shape[2]
    slab = depth // nf
    half = depth // nt
    heads = w_query.shape[1] // HD
    qcols = heads * HD
    units = w_gate.shape[1] // nc
    scale = HD ** (-0.5)

    def cut(value, start, size, axis):
        return lax.dynamic_slice_in_dim(value, start, size, axis)

    def all_to_all_blocks(blocks, axis, size):
        return [blocks[0]] + [swap(blocks[k], axis, size, k) for k in range(1, size)]

    def gather_blocks(value, axis, size):
        return [value] + [swap(value, axis, size, k) for k in range(1, size)]

    def absolute(blocks, index, axis):
        stacked = jnp.stack(blocks)
        size = len(blocks)
        return jnp.concatenate(
            [lax.dynamic_index_in_dim(stacked, j ^ index, 0, keepdims=False) for j in range(size)],
            axis=axis,
        )

    def rows_to_slabs(value):
        blocks = [cut(value, (fi ^ k) * slab, slab, 1) for k in range(nf)]
        return jnp.concatenate(all_to_all_blocks(blocks, "fsdp", nf), axis=0)

    def slabs_to_rows(value):
        blocks = list(value.reshape(nf, rows, slab))
        return absolute(all_to_all_blocks(blocks, "fsdp", nf), fi, 1)

    def reduce_rows(value, width):
        blocks = list(value.reshape(nf, rows, width))
        got = all_to_all_blocks(blocks, "fsdp", nf)
        return sum(block.astype(F32) for block in got)

    def gather_rows(value):
        return jnp.concatenate(gather_blocks(value, "fsdp", nf), axis=0)

    def both_halves(mine, axis):
        other = swap(mine, "tp", nt, 1)
        return jnp.where(
            ti == 0,
            jnp.concatenate([mine, other], axis=axis),
            jnp.concatenate([other, mine], axis=axis),
        )

    def tp_sum(value):
        low = value.astype(BF)
        return low.astype(F32) + swap(low, "tp", nt, 1).astype(F32)

    def gather_ctx(value):
        mine = cut(value, ti * half, half, 1)
        return both_halves(jnp.concatenate(gather_blocks(mine, "ctx", nc), axis=0), 1)

    def reduce_ctx(value):
        low = value.astype(BF)
        keep = cut(low, ti * half, half, 1)
        send = cut(low, (1 - ti) * half, half, 1)
        both = (keep.astype(F32) + swap(send, "tp", nt, 1).astype(F32)).astype(BF)
        got = all_to_all_blocks(list(both.reshape(nc, rows, half)), "ctx", nc)
        return sum(block.astype(F32) for block in got)

    gate_full = lax.all_gather(cut(w_gate, ci * units, units, 1), "fsdp", axis=0, tiled=True)
    up_full = lax.all_gather(cut(w_up, ci * units, units, 1), "fsdp", axis=0, tiled=True)
    down_full = lax.all_gather(
        cut(w_down, ci * units, units, 0).T, "fsdp", axis=0, tiled=True
    )

    gains = jnp.stack([gain_attn, gain_ffn])
    gains = absolute(gather_blocks(gains, "fsdp", nf), fi, 1).astype(F32)
    gain_one, gain_two = gains[0], gains[1]
    inputs = tokens[0].astype(F32)
    incoming = cotangent[0]

    segment_row = segment_ids[0]
    offset = ci * rows
    local_segment = lax.dynamic_slice_in_dim(segment_row, offset, rows, 0)
    local_index = offset + jnp.arange(rows, dtype=jnp.int32)
    earlier = jnp.sum((segment_row[None, :] < local_segment[:, None]).astype(jnp.int32), axis=1)
    position = (local_index - earlier).astype(F32)
    freqs = 10000.0 ** (-(jnp.arange(HD // 4, dtype=F32) * 2.0 / (HD // 2)))
    angle = position[:, None] * freqs[None, :]
    cosine = jnp.cos(angle)
    sine = jnp.sin(angle)

    normed_attn = rms_scale(inputs, gain_one).astype(BF)
    normed_slab = rows_to_slabs(normed_attn)
    kv_half = cut(w_keyval, ti * HD, HD, 1)
    partial = jnp.concatenate(
        [matmul(normed_slab, w_query).astype(BF), matmul(normed_slab, kv_half).astype(BF)], axis=1
    )
    projected = reduce_rows(partial, qcols + HD)
    query = projected[:, :qcols].reshape(rows, heads, HD)
    keyval = projected[:, qcols:]
    query_rows = (
        rotate(query, cosine[:, None, :], sine[:, None, :]).reshape(rows * heads, HD).astype(BF)
    )
    keyval = jnp.where(ti == 0, rotate(keyval, cosine, sine), keyval).astype(BF)
    kv_all = jnp.concatenate(gather_blocks(keyval, "ctx", nc), axis=0)
    kv_other = swap(kv_all, "tp", nt, 1)
    key_all = jnp.where(ti == 0, kv_all, kv_other)
    value_all = jnp.where(ti == 0, kv_other, kv_all)

    key_index = jnp.concatenate(
        [(ci ^ k) * rows + jnp.arange(rows, dtype=jnp.int32) for k in range(nc)]
    )
    key_segment = jnp.concatenate(
        [lax.dynamic_slice_in_dim(segment_row, (ci ^ k) * rows, rows, 0) for k in range(nc)]
    )
    row_index = jnp.repeat(local_index, heads)
    row_segment = jnp.repeat(local_segment, heads)
    mask = (row_segment[:, None] == key_segment[None, :]) & (
        key_index[None, :] <= row_index[:, None]
    )
    scores = jnp.where(mask, times_transposed(query_rows, key_all) * scale, NEGATIVE)
    peak = jnp.max(scores, axis=1, keepdims=True)
    terms = jnp.exp(scores - peak)
    probs = terms / jnp.sum(terms, axis=1, keepdims=True)
    probs_low = probs.astype(BF)
    attended = matmul(probs_low, value_all).reshape(rows, qcols).astype(BF)

    attended_plane = gather_rows(attended)
    branch = tp_sum(matmul(attended_plane, w_out)).astype(BF)
    hidden_state = inputs + slabs_to_rows(branch).astype(F32)
    normed_ffn = rms_scale(hidden_state, gain_two).astype(BF)

    normed_all = gather_ctx(normed_ffn)
    incoming_all = gather_ctx(incoming)
    gate = matmul(normed_all, gate_full)
    upward = matmul(normed_all, up_full)
    d_hidden = matmul(incoming_all, down_full)
    hidden, geglu_pull = jax.vjp(geglu, gate, upward)
    hidden = hidden.astype(BF)
    d_gate, d_up = geglu_pull(d_hidden)
    d_gate = d_gate.astype(BF)
    d_up = d_up.astype(BF)

    def finish(grad, axis):
        low = grad.astype(BF)
        blocks = [cut(low, (fi ^ k) * slab, slab, axis) for k in range(nf)]
        got = all_to_all_blocks(blocks, "fsdp", nf)
        return sum(block.astype(F32) for block in got).astype(BF)

    shard_down = finish(transposed_times(hidden, incoming_all), 1)
    grad_down = lax.all_gather(shard_down, "ctx", axis=0, tiled=True).astype(F32)
    shard_gate = finish(transposed_times(normed_all, d_gate), 0)
    grad_gate = lax.all_gather(shard_gate, "ctx", axis=0, tiled=False)
    shard_up = finish(transposed_times(normed_all, d_up), 0)
    grad_up = lax.all_gather(shard_up, "ctx", axis=0, tiled=False)

    def spread(value):
        return jnp.concatenate([value[j] for j in range(nc)], axis=1).astype(F32)

    grad_gate = spread(grad_gate)
    grad_up = spread(grad_up)

    d_normed_ffn = reduce_ctx(
        times_transposed(d_gate, gate_full) + times_transposed(d_up, up_full)
    ).astype(BF)
    d_normed_ffn = both_halves(d_normed_ffn, 1).astype(F32)
    feed = reduce_ctx(times_transposed(hidden, down_full))
    output = both_halves((cut(hidden_state, ti * half, half, 1) + feed).astype(BF), 1)

    unused, norm_pull = jax.vjp(rms_scale, hidden_state, gain_two)
    d_state_norm, grad_gain_two = norm_pull(d_normed_ffn)
    d_state = incoming.astype(F32) + d_state_norm
    d_branch_slab = rows_to_slabs(d_state.astype(BF))
    grad_out = transposed_times(attended_plane, d_branch_slab)
    d_attended = reduce_rows(times_transposed(d_branch_slab, w_out).astype(BF), qcols)
    d_attended = d_attended.astype(BF).reshape(rows * heads, HD)
    d_probs = times_transposed(d_attended, value_all)
    delta = jnp.sum(probs * d_probs, axis=1, keepdims=True)
    d_scores = (probs * (d_probs - delta)).astype(BF)
    d_rows = matmul(d_scores, key_all) * scale
    d_key = transposed_times(d_scores, query_rows) * scale
    d_value = transposed_times(probs_low, d_attended)
    d_key, d_value = d_key.astype(BF), d_value.astype(BF)
    keep = jnp.where(ti == 0, d_key, d_value)
    send = jnp.where(ti == 0, d_value, d_key)
    d_kv = (keep.astype(F32) + swap(send, "tp", nt, 1).astype(F32)).astype(BF)
    d_kv = sum(
        block.astype(F32)
        for block in all_to_all_blocks(list(d_kv.reshape(nc, rows, HD)), "ctx", nc)
    )
    d_kv = jnp.where(ti == 0, unrotate(d_kv, cosine, sine), d_kv).astype(BF)
    d_query = unrotate(d_rows.reshape(rows, heads, HD), cosine[:, None, :], sine[:, None, :])
    d_query = d_query.reshape(rows, qcols).astype(BF)
    d_plane = gather_rows(jnp.concatenate([d_query, d_kv], axis=1))
    d_query_plane = d_plane[:, :qcols]
    d_kv_plane = d_plane[:, qcols:]
    d_normed = tp_sum(
        times_transposed(d_query_plane, w_query) + times_transposed(d_kv_plane, kv_half)
    ).astype(BF)
    d_normed_attn = slabs_to_rows(d_normed).astype(F32)
    grad_query = transposed_times(normed_slab, d_query_plane)
    grad_kv = transposed_times(normed_slab, d_kv_plane)
    unused, norm_pull_one = jax.vjp(rms_scale, inputs, gain_one)
    d_input_norm, grad_gain_one = norm_pull_one(d_normed_attn)
    grad_inputs = d_state + d_input_norm

    grad_out = lax.psum(grad_out.astype(BF), "ctx").astype(F32)
    grad_query = lax.psum(grad_query.astype(BF), "ctx").astype(F32)
    grad_kv = lax.psum(grad_kv.astype(BF), "ctx")
    grad_kv = both_halves(grad_kv, 1).astype(F32)
    gain_grads = jnp.stack([grad_gain_one, grad_gain_two])
    gain_blocks = [cut(gain_grads, (fi ^ k) * slab, slab, 1) for k in range(nf)]
    gain_grads = sum(all_to_all_blocks(gain_blocks, "fsdp", nf))
    step = 1
    while step < nc:
        gain_grads = gain_grads + swap(gain_grads, "ctx", nc, step)
        step *= 2
    return (
        output[None],
        grad_inputs[None],
        grad_query,
        grad_kv,
        grad_out,
        grad_gate,
        grad_up,
        grad_down,
        gain_grads[0],
        gain_grads[1],
    )


def solution(mesh):
    sizes = (mesh.shape["fsdp"], mesh.shape["ctx"], mesh.shape["tp"])
    in_specs = (
        P("fsdp", "ctx", None),
        P("fsdp", None),
        P("fsdp", "tp"),
        P("fsdp", None),
        P("tp", "fsdp"),
        P("fsdp", "tp"),
        P("fsdp", "tp"),
        P("tp", "fsdp"),
        P("fsdp"),
        P("fsdp"),
        P("fsdp", "ctx", None),
    )
    out_specs = (
        P("fsdp", "ctx", None),
        P("fsdp", "ctx", None),
        P("fsdp", "tp"),
        P("fsdp", None),
        P("tp", "fsdp"),
        P("fsdp", "tp"),
        P("fsdp", "tp"),
        P("tp", "fsdp"),
        P("fsdp"),
        P("fsdp"),
    )

    def body(*args):
        return per_device(sizes, *args)

    return jax.shard_map(
        body, mesh=mesh, in_specs=in_specs, out_specs=out_specs, check_vma=False
    )
```

time: 2320 us -> 841 us (0.36)
  waiting for transfers between devices: 1960 us -> 516 us
  blocking collectives: 73.9 us -> 0 us
  matrix products: 153 us -> 79.3 us
  starting transfers between devices: 1.36 us -> 73 us
  other arithmetic: 35.5 us -> 85.2 us
    psum x4 -> x1, waiting for transfers between devices: 606 us -> 0.02 us  [per_device(): grad_query = lax.psum(grad_query.astype(BF), 'ctx').astype(F32)]
    all_gather x6, waiting for transfers between devices: 659 us -> 110 us  [the longest x1 66.4 us: per_device(): lax.all_gather(shard_down, 'ctx', axis=0, tiled=True).astype(F32)]
    reduce_scatter x6 -> x0, waiting for transfers between devices: 498 us -> none  [the longest x1 180 us: per_device(): lax.psum_scatter(grad_gate.astype(jnp.bfloat16), 'fsdp', scatter_dimensio...]
    ppermute x0 -> x70, waiting for transfers between devices: none -> 406 us  [swap(): return lax.ppermute(value, axis, [(i, i ^ k) for i in range(size)])]
    unnamed x20 -> x7, waiting for transfers between devices: 196 us -> 0.11 us
    ppermute x0 -> x70, starting transfers between devices: none -> 72.6 us  [swap(): return lax.ppermute(value, axis, [(i, i ^ k) for i in range(size)])]
    all_gather x4 -> x0, blocking collectives: 46.6 us -> none  [the longest x1 14.6 us: per_device(): lax.all_gather(key_local, 'ctx', axis=0, tiled=True)]
    dot_general x8, matrix products: 55.9 us -> 23.4 us  [times_transposed(): lax.dot_general(left, right, (((1,), (1,)), ((), ())), preferred_element_...]
  transfers between devices with their start and end apart: 18 -> 77, of which waited for: 17 -> 48; matrix products, arithmetic and copies ran while one was open for 7% -> 20% of each run, Pallas kernels for 0% -> 0%
where the time goes in v1:
time: 841 us; the launch traced here: 832 us
  waiting for transfers between devices  516 us (61%)
  other arithmetic  85.2 us (10%)
  matrix products  79.3 us (9%)
  starting transfers between devices  73 us (9%)
  local copies, waits for them, and re-layouts  61.8 us (7%)
  between operations  16.2 us (2%)
    ppermute x70, waiting for transfers between devices, swap(): return lax.ppermute(value, axis, [(i, i ^ k) for i in range(size)])  406 us
    ppermute x70, starting transfers between devices, swap(): return lax.ppermute(value, axis, [(i, i ^ k) for i in range(size)])  72.6 us
    all_gather x1, waiting for transfers between devices, per_device(): lax.all_gather(shard_down, 'ctx', axis=0, tiled=True).astype(F32)  66.4 us
    all_gather x1, waiting for transfers between devices, per_device(): grad_gate = lax.all_gather(shard_gate, 'ctx', axis=0, tiled=False)  43.6 us
    unnamed x191, local copies, waits for them, and re-layouts  34.2 us
    dot_general x8, matrix products, matmul(): return jnp.dot(left, right, preferred_element_type=F32)  31.9 us
    convert_element_type x2, other arithmetic, spread(): return jnp.concatenate([value[j] for j in range(nc)], axis=1).astype(F32)  24.6 us
    dot_general x8, matrix products, transposed_times(): lax.dot_general(left, right, (((0,), (0,)), ((), ())), preferred_element_...  24 us
  transfers between devices with their start and end apart: 77, of which 48 were waited for; matrix products, arithmetic and copies ran while one was open for 20% of the time, Pallas kernels for 0%

profile of v1, /device:TPU:0, one launch (start us, length us, event | category | flops | bytes accessed | tf_op | source)
XLA Modules:
  0.0 831.8 jit_solution(476660322384380501)
XLA Ops:
  25.5 8.2 collective-permute-done.5
  33.6 3.3 collective-permute-done.4
  36.9 3.5 collective-permute-done.3
  51.5 11.0 %collective-permute-done.6 = bf16[128,1536]{0,1:T(8,128)(2,1)S(1)} collective-permute-done((bf16[128,1536]{0,1:T(8,128)(2,1)}, bf16[128,1536]{0,1:T(8,128)(2,1)S(1)}, u32[]{:S(2)}, u32[]{:S(2)}) %collective-permute-start.6) | collective-permute-done | bytes 393248 | tf_op jit(solution)/shard_map/ppermute | solution.py:47
  62.5 14.2 %collective-permute-done.8 = bf16[128,1536]{0,1:T(8,128)(2,1)S(1)} collective-permute-done((bf16[128,1536]{0,1:T(8,128)(2,1)}, bf16[128,1536]{0,1:T(8,128)(2,1)S(1)}, u32[]{:S(2)}, u32[]{:S(2)}) %collective-permute-start.8) | collective-permute-done | bytes 393248 | tf_op jit(solution)/shard_map/ppermute | solution.py:47
  78.2 3.4 collective-permute-start.11
  97.3 6.7 collective-permute-done.13
  104.0 11.3 %collective-permute-done.14 = bf16[128,1280]{1,0:T(8,128)(2,1)S(1)} collective-permute-done((bf16[128,1280]{1,0:T(8,128)(2,1)S(1)}, bf16[128,1280]{1,0:T(8,128)(2,1)S(1)}, u32[]{:S(2)}, u32[]{:S(2)}) %collective-permute-start.14) | collective-permute-done | bytes 327712 | tf_op jit(solution)/shard_map/ppermute | solution.py:47
  126.0 4.1 collective-permute-done.19
  130.1 3.5 collective-permute-done.18
  139.8 8.1 collective-permute-done.22
  148.0 18.5 %collective-permute-done.21 = bf16[128,1280]{1,0:T(8,128)(2,1)S(1)} collective-permute-done((bf16[128,1280]{1,0:T(8,128)(2,1)S(1)}, bf16[128,1280]{1,0:T(8,128)(2,1)S(1)}, u32[]{:S(2)}, u32[]{:S(2)}) %collective-permute-start.21) | collective-permute-done | bytes 327712 | tf_op jit(solution)/shard_map/ppermute | solution.py:47
  173.0 8.4 %collective-permute-done.31 = bf16[128,1280]{1,0:T(8,128)(2,1)} collective-permute-done((bf16[128,1280]{1,0:T(8,128)(2,1)}, bf16[128,1280]{1,0:T(8,128)(2,1)}, u32[]{:S(2)}, u32[]{:S(2)}) %collective-permute-start.31) | collective-permute-done | bytes 327712 | tf_op jit(solution)/shard_map/ppermute | solution.py:47
  181.5 17.9 %collective-permute-done.30 = bf16[128,1280]{1,0:T(8,128)(2,1)} collective-permute-done((bf16[128,1280]{1,0:T(8,128)(2,1)}, bf16[128,1280]{1,0:T(8,128)(2,1)}, u32[]{:S(2)}, u32[]{:S(2)}) %collective-permute-start.30) | collective-permute-done | bytes 327712 | tf_op jit(solution)/shard_map/ppermute | solution.py:47
  201.8 19.2 %maximum_select_fusion = bf16[512,2560]{1,0:T(8,128)(2,1)} fusion(bf16[512,1280]{1,0:T(8,128)(2,1)} %collective-permute-done.23, bf16[128,1280]{1,0:T(8,128)(2,1)S(1)} %copy-done.23, bf16[128,1280]{1,0:T(8,128)(2,1)S(1)} %copy-done.25, bf16[128,1280]{1,0:T(8,128)(2,1)S(1)} %copy-done.27, bf16[128,1280]{1,0:T(8,128)(2,1)S(1)} %fusion.31, pred[]{:T(512)S(6)} %eq.10), kind=kLoop, calls=%fused_computation.13 | loop fusion | flops 27525120 | bytes 5242881 | tf_op jit(solution)/shard_map/jit(_where)/select_n | solution.py:110
  221.0 7.3 fusion.85
  228.3 7.3 fusion.84
  235.7 10.6 %multiply_convert_fusion = (bf16[512,960]{0,1:T(8,128)(2,1)S(1)}, bf16[512,960]{0,1:T(8,128)(2,1)S(1)}, bf16[512,960]{0,1:T(8,128)(2,1)}) fusion(f32[512,960]{0,1:T(8,128)} %fusion.84, f32[512,960]{0,1:T(8,128)} %fusion.85, bf16[2560,960]{0,1:T(8,128)(2,1)} %all-gather.13.cloned.1.call-done, bf16[512,1280]{1,0:T(8,128)(2,1)} %collective-permute-done.32, ...), kind=kOutput, calls=%fused_computation.40 | convolution fusion | flops 2556887040 | bytes 14417921 | tf_op jit(solution)/shard_map/dot_general | solution.py:31
  249.3 6.3 add_convert_fusion
  262.9 13.3 %collective-permute-done.34 = bf16[128,1280]{1,0:T(8,128)(2,1)S(1)} collective-permute-done((bf16[128,1280]{1,0:T(8,128)(2,1)S(1)}, bf16[128,1280]{1,0:T(8,128)(2,1)S(1)}, u32[]{:S(2)}, u32[]{:S(2)}) %collective-permute-start.34) | collective-permute-done | bytes 327712 | tf_op jit(solution)/shard_map/ppermute | solution.py:47
  276.7 15.0 %collective-permute-done.35 = bf16[128,1280]{1,0:T(8,128)(2,1)S(1)} collective-permute-done((bf16[128,1280]{1,0:T(8,128)(2,1)S(1)}, bf16[128,1280]{1,0:T(8,128)(2,1)S(1)}, u32[]{:S(2)}, u32[]{:S(2)}) %collective-permute-start.35) | collective-permute-done | bytes 327712 | tf_op jit(solution)/shard_map/ppermute | solution.py:47
  300.0 4.5 collective-permute-done.40
  312.1 7.1 collective-permute-done.41
  319.2 6.5 collective-permute-done.43
  346.5 3.5 collective-permute-done.46
  355.4 3.4 convolution_convert_fusion.4
  358.8 6.0 collective-permute-done.50
  364.9 7.5 collective-permute-done.49
  378.3 4.8 convolution_convert_fusion
  387.0 26.4 %collective-permute-done.59 = bf16[640,960]{0,1:T(8,128)(2,1)S(1)} collective-permute-done((bf16[640,960]{0,1:T(8,128)(2,1)S(1)}, bf16[640,960]{0,1:T(8,128)(2,1)S(1)}, u32[]{:S(2)}, u32[]{:S(2)}) %collective-permute-start.59) | collective-permute-done | bytes 1228832 | tf_op jit(solution)/shard_map/ppermute | solution.py:47
  413.4 26.0 %collective-permute-done.61 = bf16[640,960]{0,1:T(8,128)(2,1)S(1)} collective-permute-done((bf16[640,960]{0,1:T(8,128)(2,1)S(1)}, bf16[640,960]{0,1:T(8,128)(2,1)S(1)}, u32[]{:S(2)}, u32[]{:S(2)}) %collective-permute-start.61) | collective-permute-done | bytes 1228832 | tf_op jit(solution)/shard_map/ppermute | solution.py:47
  442.6 4.8 convolution_convert_fusion.1
  451.3 26.4 %collective-permute-done.56 = bf16[640,960]{0,1:T(8,128)(2,1)S(1)} collective-permute-done((bf16[640,960]{0,1:T(8,128)(2,1)S(1)}, bf16[640,960]{0,1:T(8,128)(2,1)S(1)}, u32[]{:S(2)}, u32[]{:S(2)}) %collective-permute-start.56) | collective-permute-done | bytes 1228832 | tf_op jit(solution)/shard_map/ppermute | solution.py:47
  477.7 23.7 %collective-permute-done.58 = bf16[640,960]{0,1:T(8,128)(2,1)S(1)} collective-permute-done((bf16[640,960]{0,1:T(8,128)(2,1)S(1)}, bf16[640,960]{0,1:T(8,128)(2,1)S(1)}, u32[]{:S(2)}, u32[]{:S(2)}) %collective-permute-start.58) | collective-permute-done | bytes 1228832 | tf_op jit(solution)/shard_map/ppermute | solution.py:47
  504.5 5.8 convolution_convert_fusion.2
  514.2 5.7 convolution_convert_fusion.3
  521.9 18.7 %collective-permute-done.62 = bf16[960,640]{1,0:T(8,128)(2,1)S(1)} collective-permute-done((bf16[960,640]{1,0:T(8,128)(2,1)S(1)}, bf16[960,640]{1,0:T(8,128)(2,1)S(1)}, u32[]{:S(2)}, u32[]{:S(2)}) %collective-permute-start.62) | collective-permute-done | bytes 1228832 | tf_op jit(solution)/shard_map/ppermute | solution.py:47
  540.6 21.7 %collective-permute-done.64 = bf16[960,640]{1,0:T(8,128)(2,1)S(1)} collective-permute-done((bf16[960,640]{1,0:T(8,128)(2,1)S(1)}, bf16[960,640]{1,0:T(8,128)(2,1)S(1)}, u32[]{:S(2)}, u32[]{:S(2)}) %collective-permute-start.64) | collective-permute-done | bytes 1228832 | tf_op jit(solution)/shard_map/ppermute | solution.py:47
  577.7 25.3 %collective-permute-done.25 = bf16[128,1280]{1,0:T(8,128)(2,1)S(1)} collective-permute-done((bf16[128,1280]{1,0:T(8,128)(2,1)S(1)}, bf16[128,1280]{1,0:T(8,128)(2,1)S(1)}, u32[]{:S(2)}, u32[]{:S(2)}) %collective-permute-start.25) | collective-permute-done | bytes 327712 | tf_op jit(solution)/shard_map/ppermute | solution.py:47
  603.9 27.7 %collective-permute-done.26 = bf16[128,1280]{1,0:T(8,128)(2,1)S(1)} collective-permute-done((bf16[128,1280]{1,0:T(8,128)(2,1)S(1)}, bf16[128,1280]{1,0:T(8,128)(2,1)S(1)}, u32[]{:S(2)}, u32[]{:S(2)}) %collective-permute-start.26) | collective-permute-done | bytes 327712 | tf_op jit(solution)/shard_map/ppermute | solution.py:47
  640.7 3.6 collective-permute-done.68
  658.0 12.5 %maximum_convert_fusion.1 = f32[640,3840]{0,1:T(8,128)} fusion(bf16[640,960]{0,1:T(8,128)(2,1)S(1)} %get-tuple-element.67, bf16[640,960]{0,1:T(8,128)(2,1)S(1)} %get-tuple-element.65, bf16[640,960]{0,1:T(8,128)(2,1)S(1)} %get-tuple-element.66, bf16[640,960]{0,1:T(8,128)(2,1)S(1)} %get-tuple-element.64), kind=kLoop, calls=%fused_computation.5 | loop fusion | flops 19660800 | bytes 14745600 | tf_op jit(solution)/shard_map/convert_element_type | solution.py:221
  670.4 11.0 %copy.66 = f32[640,3840]{1,0:T(8,128)} copy(f32[640,3840]{0,1:T(8,128)} %maximum_convert_fusion.1) | data formatting | bytes 19660800
  681.5 43.6 %all-gather.17.cloned.1.call-done = bf16[2560,960]{0,1:T(8,128)(2,1)} async-done(((bf16[640,960]{0,1:T(8,128)(2,1)}), bf16[2560,960]{0,1:T(8,128)(2,1)}) %all-gather.17.cloned.1.call-update) | async-done | bytes 4915216 | tf_op jit(solution)/shard_map/all_gather | solution.py:216
  727.9 12.2 %maximum_convert_fusion = f32[640,3840]{0,1:T(8,128)} fusion(bf16[640,960]{0,1:T(8,128)(2,1)S(1)} %get-tuple-element.74, bf16[640,960]{0,1:T(8,128)(2,1)S(1)} %get-tuple-element.72, bf16[640,960]{0,1:T(8,128)(2,1)S(1)} %get-tuple-element.73, bf16[640,960]{0,1:T(8,128)(2,1)S(1)} %get-tuple-element.71), kind=kLoop, calls=%fused_computation.4 | loop fusion | flops 19660800 | bytes 14745600 | tf_op jit(solution)/shard_map/convert_element_type | solution.py:221
  740.1 11.0 %copy.65 = f32[640,3840]{1,0:T(8,128)} copy(f32[640,3840]{0,1:T(8,128)} %maximum_convert_fusion) | data formatting | bytes 19660800
  751.1 66.4 %all-gather.15.cloned.1.call-done = bf16[3840,640]{1,0:T(8,128)(2,1)} async-done(((bf16[960,640]{1,0:T(8,128)(2,1)}), bf16[3840,640]{1,0:T(8,128)(2,1)}) %all-gather.15.cloned.1.call-update) | async-done | bytes 4915216 | tf_op jit(solution)/shard_map/all_gather | solution.py:214
  817.5 7.0 convert_element_type.435
  (447 shorter events, 191.6 us)
Async XLA Ops:
  7.2 213.8 %all-gather.11.cloned.1.call-start = ((), (), s32[]{:S(2)}) async-start(), calls=%async_computation.1 | async-start | bytes 6553600 | tf_op jit(solution)/shard_map/all_gather | solution.py:133
  10.4 217.9 %all-gather.9.cloned.1.call-start = ((), (), s32[]{:S(2)}) async-start(), calls=%async_computation | async-start | bytes 6553600 | tf_op jit(solution)/shard_map/all_gather | solution.py:132
  18.8 216.9 %all-gather.13.cloned.1.call-start = ((), (), s32[]{:S(2)}) async-start(), calls=%async_computation.2 | async-start | bytes 6144000 | tf_op jit(solution)/shard_map/all_gather | solution.py:134
  21.9 11.7 %collective-permute-start.5 = (bf16[128,640]{1,0:T(8,128)(2,1)}, bf16[128,640]{1,0:T(8,128)(2,1)S(1)}, u32[]{:S(2)}, u32[]{:S(2)}) collective-permute-start(bf16[128,640]{1,0:T(8,128)(2,1)} %get-tuple-element.122), channel_id=1, source_target_pairs={{0,24},{8,16},{16,8},{24,0},{1,25},{9,17},{17,9},{25,1},{2,26},{10... | collective-permute-start | bytes 491528 | tf_op jit(solution)/shard_map/ppermute | solution.py:47
  24.8 12.1 %collective-permute-start.4 = (bf16[128,640]{1,0:T(8,128)(2,1)S(1)}, bf16[128,640]{1,0:T(8,128)(2,1)S(1)}, u32[]{:S(2)}, u32[]{:S(2)}) collective-permute-start(bf16[128,640]{1,0:T(8,128)(2,1)S(1)} %get-tuple-element.123), channel_id=1, source_target_pairs={{0,16},{8,24},{16,0},{24,8},{1,17},{9,25},{17,1},{25,9},{2,18},{10... | collective-permute-start | bytes 491528 | tf_op jit(solution)/shard_map/ppermute | solution.py:47
  25.3 15.1 %collective-permute-start.3 = (bf16[128,640]{1,0:T(8,128)(2,1)S(1)}, bf16[128,640]{1,0:T(8,128)(2,1)S(1)}, u32[]{:S(2)}, u32[]{:S(2)}) collective-permute-start(bf16[128,640]{1,0:T(8,128)(2,1)S(1)} %get-tuple-element.124), channel_id=1, source_target_pairs={{0,8},{8,0},{16,24},{24,16},{1,9},{9,1},{17,25},{25,17},{2,10},{10... | collective-permute-start | bytes 491528 | tf_op jit(solution)/shard_map/ppermute | solution.py:47
  45.4 17.1 %collective-permute-start.6 = (bf16[128,1536]{0,1:T(8,128)(2,1)}, bf16[128,1536]{0,1:T(8,128)(2,1)S(1)}, u32[]{:S(2)}, u32[]{:S(2)}) collective-permute-start(bf16[128,1536]{0,1:T(8,128)(2,1)} %get-tuple-element.81), channel_id=1, source_target_pairs={{0,8},{8,0},{16,24},{24,16},{1,9},{9,1},{17,25},{25,17},{2,10},{10... | collective-permute-start | bytes 1179656 | tf_op jit(solution)/shard_map/ppermute | solution.py:47
  47.0 29.6 %collective-permute-start.8 = (bf16[128,1536]{0,1:T(8,128)(2,1)}, bf16[128,1536]{0,1:T(8,128)(2,1)S(1)}, u32[]{:S(2)}, u32[]{:S(2)}) collective-permute-start(bf16[128,1536]{0,1:T(8,128)(2,1)} %get-tuple-element.82), channel_id=1, source_target_pairs={{0,24},{8,16},{16,8},{24,0},{1,25},{9,17},{17,9},{25,1},{2,26},{10... | collective-permute-start | bytes 1179656 | tf_op jit(solution)/shard_map/ppermute | solution.py:47
  47.0 29.6 %collective-permute-start.7 = (bf16[128,1536]{0,1:T(8,128)(2,1)}, bf16[128,1536]{0,1:T(8,128)(2,1)}, u32[]{:S(2)}, u32[]{:S(2)}) collective-permute-start(bf16[128,1536]{0,1:T(8,128)(2,1)} %get-tuple-element.83), channel_id=1, source_target_pairs={{0,16},{8,24},{16,0},{24,8},{1,17},{9,25},{17,1},{25,9},{2,18},{10... | collective-permute-start | bytes 1179656 | tf_op jit(solution)/shard_map/ppermute | solution.py:47
  94.4 20.9 %collective-permute-start.15 = (bf16[128,1280]{1,0:T(8,128)(2,1)S(1)}, bf16[128,1280]{1,0:T(8,128)(2,1)S(1)}, u32[]{:S(2)}, u32[]{:S(2)}) collective-permute-start(bf16[128,1280]{1,0:T(8,128)(2,1)S(1)} %convert_element_type.349), channel_id=1, source_target_pairs={{0,24},{8,16},{16,8},{24,0},{1,25},{9,17},{17,9},{25,1},{2,26},{10... | collective-permute-start | bytes 983048 | tf_op jit(solution)/shard_map/ppermute | solution.py:47
  96.8 18.5 %collective-permute-start.14 = (bf16[128,1280]{1,0:T(8,128)(2,1)S(1)}, bf16[128,1280]{1,0:T(8,128)(2,1)S(1)}, u32[]{:S(2)}, u32[]{:S(2)}) collective-permute-start(bf16[128,1280]{1,0:T(8,128)(2,1)S(1)} %convert_element_type.349), channel_id=1, source_target_pairs={{0,16},{8,24},{16,0},{24,8},{1,17},{9,25},{17,1},{25,9},{2,18},{10... | collective-permute-start | bytes 983048 | tf_op jit(solution)/shard_map/ppermute | solution.py:47
  119.4 524.9 %all-reduce.3.cloned.1.call-start = ((), (), s32[]{:S(2)}) async-start(), calls=%async_computation.6 | async-start | bytes 7208960 | tf_op jit(solution)/shard_map/psum | solution.py:271
  135.4 12.6 %collective-permute-start.22 = (bf16[128,1280]{1,0:T(8,128)(2,1)S(1)}, bf16[128,1280]{1,0:T(8,128)(2,1)S(1)}, u32[]{:S(2)}, u32[]{:S(2)}) collective-permute-start(bf16[128,1280]{1,0:T(8,128)(2,1)S(1)} %fusion.31), channel_id=1, source_target_pairs={{0,6},{2,4},{4,2},{6,0},{1,7},{3,5},{5,3},{7,1},{8,14},{10,12},{12... | collective-permute-start | bytes 983048 | tf_op jit(solution)/shard_map/ppermute | solution.py:47
  137.3 29.2 %collective-permute-start.21 = (bf16[128,1280]{1,0:T(8,128)(2,1)S(1)}, bf16[128,1280]{1,0:T(8,128)(2,1)S(1)}, u32[]{:S(2)}, u32[]{:S(2)}) collective-permute-start(bf16[128,1280]{1,0:T(8,128)(2,1)S(1)} %fusion.31), channel_id=1, source_target_pairs={{0,4},{2,6},{4,0},{6,2},{1,5},{3,7},{5,1},{7,3},{8,12},{10,14},{12... | collective-permute-start | bytes 983048 | tf_op jit(solution)/shard_map/ppermute | solution.py:47
  137.5 29.0 %collective-permute-start.20 = (bf16[128,1280]{1,0:T(8,128)(2,1)S(1)}, bf16[128,1280]{1,0:T(8,128)(2,1)S(1)}, u32[]{:S(2)}, u32[]{:S(2)}) collective-permute-start(bf16[128,1280]{1,0:T(8,128)(2,1)S(1)} %fusion.31), channel_id=1, source_target_pairs={{0,2},{2,0},{4,6},{6,4},{1,3},{3,1},{5,7},{7,5},{8,10},{10,8},{12,... | collective-permute-start | bytes 983048 | tf_op jit(solution)/shard_map/ppermute | solution.py:47
  167.8 34.0 %collective-permute-start.23 = (bf16[512,1280]{1,0:T(8,128)(2,1)}, bf16[512,1280]{1,0:T(8,128)(2,1)}, u32[]{:S(2)}, u32[]{:S(2)}) collective-permute-start(bf16[512,1280]{1,0:T(8,128)(2,1)} %pad_maximum_fusion.1), channel_id=1, source_target_pairs={{0,1},{1,0},{2,3},{3,2},{4,5},{5,4},{6,7},{7,6},{8,9},{9,8},{10,11... | collective-permute-start | bytes 3932168 | tf_op jit(solution)/shard_map/ppermute | solution.py:47
  168.6 12.8 %collective-permute-start.31 = (bf16[128,1280]{1,0:T(8,128)(2,1)}, bf16[128,1280]{1,0:T(8,128)(2,1)}, u32[]{:S(2)}, u32[]{:S(2)}) collective-permute-start(bf16[128,1280]{1,0:T(8,128)(2,1)} %dynamic-slice_bitcast_fusion.1), channel_id=1, source_target_pairs={{0,6},{2,4},{4,2},{6,0},{1,7},{3,5},{5,3},{7,1},{8,14},{10,12},{12... | collective-permute-start | bytes 983048 | tf_op jit(solution)/shard_map/ppermute | solution.py:47
  171.3 28.1 %collective-permute-start.30 = (bf16[128,1280]{1,0:T(8,128)(2,1)}, bf16[128,1280]{1,0:T(8,128)(2,1)}, u32[]{:S(2)}, u32[]{:S(2)}) collective-permute-start(bf16[128,1280]{1,0:T(8,128)(2,1)} %dynamic-slice_bitcast_fusion.1), channel_id=1, source_target_pairs={{0,4},{2,6},{4,0},{6,2},{1,5},{3,7},{5,1},{7,3},{8,12},{10,14},{12... | collective-permute-start | bytes 983048 | tf_op jit(solution)/shard_map/ppermute | solution.py:47
  171.3 28.1 %collective-permute-start.29 = (bf16[128,1280]{1,0:T(8,128)(2,1)}, bf16[128,1280]{1,0:T(8,128)(2,1)}, u32[]{:S(2)}, u32[]{:S(2)}) collective-permute-start(bf16[128,1280]{1,0:T(8,128)(2,1)} %dynamic-slice_bitcast_fusion.1), channel_id=1, source_target_pairs={{0,2},{2,0},{4,6},{6,4},{1,3},{3,1},{5,7},{7,5},{8,10},{10,8},{12,... | collective-permute-start | bytes 983048 | tf_op jit(solution)/shard_map/ppermute | solution.py:47
  201.8 33.9 %collective-permute-start.32 = (bf16[512,1280]{1,0:T(8,128)(2,1)}, bf16[512,1280]{1,0:T(8,128)(2,1)}, u32[]{:S(2)}, u32[]{:S(2)}) collective-permute-start(bf16[512,1280]{1,0:T(8,128)(2,1)} %pad_maximum_fusion.2), channel_id=1, source_target_pairs={{0,1},{1,0},{2,3},{3,2},{4,5},{5,4},{6,7},{7,6},{8,9},{9,8},{10,11... | collective-permute-start | bytes 3932168 | tf_op jit(solution)/shard_map/ppermute | solution.py:47
  259.3 16.8 %collective-permute-start.34 = (bf16[128,1280]{1,0:T(8,128)(2,1)S(1)}, bf16[128,1280]{1,0:T(8,128)(2,1)S(1)}, u32[]{:S(2)}, u32[]{:S(2)}) collective-permute-start(bf16[128,1280]{1,0:T(8,128)(2,1)S(1)} %get-tuple-element.89), channel_id=1, source_target_pairs={{0,2},{2,0},{4,6},{6,4},{1,3},{3,1},{5,7},{7,5},{8,10},{10,8},{12,... | collective-permute-start | bytes 983048 | tf_op jit(solution)/shard_map/ppermute | solution.py:47
  259.4 17.3 %collective-permute-start.36 = (bf16[128,1280]{1,0:T(8,128)(2,1)S(1)}, bf16[128,1280]{1,0:T(8,128)(2,1)S(1)}, u32[]{:S(2)}, u32[]{:S(2)}) collective-permute-start(bf16[128,1280]{1,0:T(8,128)(2,1)S(1)} %get-tuple-element.90), channel_id=1, source_target_pairs={{0,6},{2,4},{4,2},{6,0},{1,7},{3,5},{5,3},{7,1},{8,14},{10,12},{12... | collective-permute-start | bytes 983048 | tf_op jit(solution)/shard_map/ppermute | solution.py:47
  261.1 30.6 %collective-permute-start.35 = (bf16[128,1280]{1,0:T(8,128)(2,1)S(1)}, bf16[128,1280]{1,0:T(8,128)(2,1)S(1)}, u32[]{:S(2)}, u32[]{:S(2)}) collective-permute-start(bf16[128,1280]{1,0:T(8,128)(2,1)S(1)} %get-tuple-element.91), channel_id=1, source_target_pairs={{0,4},{2,6},{4,0},{6,2},{1,5},{3,7},{5,1},{7,3},{8,12},{10,14},{12... | collective-permute-start | bytes 983048 | tf_op jit(solution)/shard_map/ppermute | solution.py:47
  308.5 10.7 %collective-permute-start.41 = (bf16[128,1280]{1,0:T(8,128)(2,1)S(1)}, bf16[128,1280]{1,0:T(8,128)(2,1)S(1)}, u32[]{:S(2)}, u32[]{:S(2)}) collective-permute-start(bf16[128,1280]{1,0:T(8,128)(2,1)S(1)} %get-tuple-element.84), channel_id=1, source_target_pairs={{0,8},{8,0},{16,24},{24,16},{1,9},{9,1},{17,25},{25,17},{2,10},{10... | collective-permute-start | bytes 983048 | tf_op jit(solution)/shard_map/ppermute | solution.py:47
  309.8 15.9 %collective-permute-start.43 = (bf16[128,1280]{1,0:T(8,128)(2,1)S(1)}, bf16[128,1280]{1,0:T(8,128)(2,1)S(1)}, u32[]{:S(2)}, u32[]{:S(2)}) collective-permute-start(bf16[128,1280]{1,0:T(8,128)(2,1)S(1)} %get-tuple-element.85), channel_id=1, source_target_pairs={{0,24},{8,16},{16,8},{24,0},{1,25},{9,17},{17,9},{25,1},{2,26},{10... | collective-permute-start | bytes 983048 | tf_op jit(solution)/shard_map/ppermute | solution.py:47
  311.0 16.1 %collective-permute-start.42 = (bf16[128,1280]{1,0:T(8,128)(2,1)S(1)}, bf16[128,1280]{1,0:T(8,128)(2,1)S(1)}, u32[]{:S(2)}, u32[]{:S(2)}) collective-permute-start(bf16[128,1280]{1,0:T(8,128)(2,1)S(1)} %get-tuple-element.86), channel_id=1, source_target_pairs={{0,16},{8,24},{16,0},{24,8},{1,17},{9,25},{17,1},{25,9},{2,18},{10... | collective-permute-start | bytes 983048 | tf_op jit(solution)/shard_map/ppermute | solution.py:47
  351.9 13.0 %collective-permute-start.50 = (bf16[128,1536]{0,1:T(8,128)(2,1)S(1)}, bf16[128,1536]{0,1:T(8,128)(2,1)S(1)}, u32[]{:S(2)}, u32[]{:S(2)}) collective-permute-start(bf16[128,1536]{0,1:T(8,128)(2,1)S(1)} %pad_maximum_fusion.10), channel_id=1, source_target_pairs={{0,24},{8,16},{16,8},{24,0},{1,25},{9,17},{17,9},{25,1},{2,26},{10... | collective-permute-start | bytes 1179656 | tf_op jit(solution)/shard_map/ppermute | solution.py:47
  353.3 19.1 %collective-permute-start.49 = (bf16[128,1536]{0,1:T(8,128)(2,1)S(1)}, bf16[128,1536]{0,1:T(8,128)(2,1)S(1)}, u32[]{:S(2)}, u32[]{:S(2)}) collective-permute-start(bf16[128,1536]{0,1:T(8,128)(2,1)S(1)} %pad_maximum_fusion.10), channel_id=1, source_target_pairs={{0,16},{8,24},{16,0},{24,8},{1,17},{9,25},{17,1},{25,9},{2,18},{10... | collective-permute-start | bytes 1179656 | tf_op jit(solution)/shard_map/ppermute | solution.py:47
  354.3 18.1 %collective-permute-start.48 = (bf16[128,1536]{0,1:T(8,128)(2,1)S(1)}, bf16[128,1536]{0,1:T(8,128)(2,1)S(1)}, u32[]{:S(2)}, u32[]{:S(2)}) collective-permute-start(bf16[128,1536]{0,1:T(8,128)(2,1)S(1)} %pad_maximum_fusion.10), channel_id=1, source_target_pairs={{0,8},{8,0},{16,24},{24,16},{1,9},{9,1},{17,25},{25,17},{2,10},{10... | collective-permute-start | bytes 1179656 | tf_op jit(solution)/shard_map/ppermute | solution.py:47
  377.1 278.0 %all-gather.19.cloned.1.call-start = ((), (), s32[]{:S(2)}) async-start(), calls=%async_computation.5 | async-start | bytes 6144000 | tf_op jit(solution)/shard_map/all_gather | solution.py:218
  383.4 30.0 %collective-permute-start.59 = (bf16[640,960]{0,1:T(8,128)(2,1)S(1)}, bf16[640,960]{0,1:T(8,128)(2,1)S(1)}, u32[]{:S(2)}, u32[]{:S(2)}) collective-permute-start(bf16[640,960]{0,1:T(8,128)(2,1)S(1)} %get-tuple-element.68), channel_id=1, source_target_pairs={{0,8},{8,0},{16,24},{24,16},{1,9},{9,1},{17,25},{25,17},{2,10},{10... | collective-permute-start | bytes 3686408 | tf_op jit(solution)/shard_map/ppermute | solution.py:47
  384.4 55.0 %collective-permute-start.61 = (bf16[640,960]{0,1:T(8,128)(2,1)S(1)}, bf16[640,960]{0,1:T(8,128)(2,1)S(1)}, u32[]{:S(2)}, u32[]{:S(2)}) collective-permute-start(bf16[640,960]{0,1:T(8,128)(2,1)S(1)} %get-tuple-element.69), channel_id=1, source_target_pairs={{0,24},{8,16},{16,8},{24,0},{1,25},{9,17},{17,9},{25,1},{2,26},{10... | collective-permute-start | bytes 3686408 | tf_op jit(solution)/shard_map/ppermute | solution.py:47
  386.1 54.7 %collective-permute-start.60 = (bf16[640,960]{0,1:T(8,128)(2,1)S(1)}, bf16[640,960]{0,1:T(8,128)(2,1)S(1)}, u32[]{:S(2)}, u32[]{:S(2)}) collective-permute-start(bf16[640,960]{0,1:T(8,128)(2,1)S(1)} %get-tuple-element.70), channel_id=1, source_target_pairs={{0,16},{8,24},{16,0},{24,8},{1,17},{9,25},{17,1},{25,9},{2,18},{10... | collective-permute-start | bytes 3686408 | tf_op jit(solution)/shard_map/ppermute | solution.py:47
  442.6 282.5 %all-gather.17.cloned.1.call-start = ((), (), s32[]{:S(2)}) async-start(), calls=%async_computation.4 | async-start | bytes 6144000 | tf_op jit(solution)/shard_map/all_gather | solution.py:216
  447.8 30.0 %collective-permute-start.56 = (bf16[640,960]{0,1:T(8,128)(2,1)S(1)}, bf16[640,960]{0,1:T(8,128)(2,1)S(1)}, u32[]{:S(2)}, u32[]{:S(2)}) collective-permute-start(bf16[640,960]{0,1:T(8,128)(2,1)S(1)} %get-tuple-element.75), channel_id=1, source_target_pairs={{0,8},{8,0},{16,24},{24,16},{1,9},{9,1},{17,25},{25,17},{2,10},{10... | collective-permute-start | bytes 3686408 | tf_op jit(solution)/shard_map/ppermute | solution.py:47
  448.7 52.7 %collective-permute-start.58 = (bf16[640,960]{0,1:T(8,128)(2,1)S(1)}, bf16[640,960]{0,1:T(8,128)(2,1)S(1)}, u32[]{:S(2)}, u32[]{:S(2)}) collective-permute-start(bf16[640,960]{0,1:T(8,128)(2,1)S(1)} %get-tuple-element.76), channel_id=1, source_target_pairs={{0,24},{8,16},{16,8},{24,0},{1,25},{9,17},{17,9},{25,1},{2,26},{10... | collective-permute-start | bytes 3686408 | tf_op jit(solution)/shard_map/ppermute | solution.py:47
  450.3 52.5 %collective-permute-start.57 = (bf16[640,960]{0,1:T(8,128)(2,1)S(1)}, bf16[640,960]{0,1:T(8,128)(2,1)S(1)}, u32[]{:S(2)}, u32[]{:S(2)}) collective-permute-start(bf16[640,960]{0,1:T(8,128)(2,1)S(1)} %get-tuple-element.77), channel_id=1, source_target_pairs={{0,16},{8,24},{16,0},{24,8},{1,17},{9,25},{17,1},{25,9},{2,18},{10... | collective-permute-start | bytes 3686408 | tf_op jit(solution)/shard_map/ppermute | solution.py:47
  504.5 313.0 %all-gather.15.cloned.1.call-start = ((), (), s32[]{:S(2)}) async-start(), calls=%async_computation.3 | async-start | bytes 6144000 | tf_op jit(solution)/shard_map/all_gather | solution.py:214
  510.7 30.0 %collective-permute-start.62 = (bf16[960,640]{1,0:T(8,128)(2,1)S(1)}, bf16[960,640]{1,0:T(8,128)(2,1)S(1)}, u32[]{:S(2)}, u32[]{:S(2)}) collective-permute-start(bf16[960,640]{1,0:T(8,128)(2,1)S(1)} %get-tuple-element.61), channel_id=1, source_target_pairs={{0,8},{8,0},{16,24},{24,16},{1,9},{9,1},{17,25},{25,17},{2,10},{10... | collective-permute-start | bytes 3686408 | tf_op jit(solution)/shard_map/ppermute | solution.py:47
  511.6 50.7 %collective-permute-start.64 = (bf16[960,640]{1,0:T(8,128)(2,1)S(1)}, bf16[960,640]{1,0:T(8,128)(2,1)S(1)}, u32[]{:S(2)}, u32[]{:S(2)}) collective-permute-start(bf16[960,640]{1,0:T(8,128)(2,1)S(1)} %get-tuple-element.62), channel_id=1, source_target_pairs={{0,24},{8,16},{16,8},{24,0},{1,25},{9,17},{17,9},{25,1},{2,26},{10... | collective-permute-start | bytes 3686408 | tf_op jit(solution)/shard_map/ppermute | solution.py:47
  513.3 50.4 %collective-permute-start.63 = (bf16[960,640]{1,0:T(8,128)(2,1)S(1)}, bf16[960,640]{1,0:T(8,128)(2,1)S(1)}, u32[]{:S(2)}, u32[]{:S(2)}) collective-permute-start(bf16[960,640]{1,0:T(8,128)(2,1)S(1)} %get-tuple-element.63), channel_id=1, source_target_pairs={{0,16},{8,24},{16,0},{24,8},{1,17},{9,25},{17,1},{25,9},{2,18},{10... | collective-permute-start | bytes 3686408 | tf_op jit(solution)/shard_map/ppermute | solution.py:47
  521.9 48.0 %collective-permute-start.24 = (bf16[512,1280]{1,0:T(8,128)(2,1)}, bf16[512,1280]{1,0:T(8,128)(2,1)}, u32[]{:S(2)}, u32[]{:S(2)}) collective-permute-start(bf16[512,1280]{1,0:T(8,128)(2,1)} %constant_dynamic-slice_fusion.18), channel_id=1, source_target_pairs={{0,1},{1,0},{2,3},{3,2},{4,5},{5,4},{6,7},{7,6},{8,9},{9,8},{10,11... | collective-permute-start | bytes 3932168 | tf_op jit(solution)/shard_map/ppermute | solution.py:47
  571.6 31.4 %collective-permute-start.25 = (bf16[128,1280]{1,0:T(8,128)(2,1)S(1)}, bf16[128,1280]{1,0:T(8,128)(2,1)S(1)}, u32[]{:S(2)}, u32[]{:S(2)}) collective-permute-start(bf16[128,1280]{1,0:T(8,128)(2,1)S(1)} %get-tuple-element.92), channel_id=1, source_target_pairs={{0,2},{2,0},{4,6},{6,4},{1,3},{3,1},{5,7},{7,5},{8,10},{10,8},{12,... | collective-permute-start | bytes 983048 | tf_op jit(solution)/shard_map/ppermute | solution.py:47
  571.7 32.2 %collective-permute-start.27 = (bf16[128,1280]{1,0:T(8,128)(2,1)S(1)}, bf16[128,1280]{1,0:T(8,128)(2,1)S(1)}, u32[]{:S(2)}, u32[]{:S(2)}) collective-permute-start(bf16[128,1280]{1,0:T(8,128)(2,1)S(1)} %get-tuple-element.93), channel_id=1, source_target_pairs={{0,6},{2,4},{4,2},{6,0},{1,7},{3,5},{5,3},{7,1},{8,14},{10,12},{12... | collective-permute-start | bytes 983048 | tf_op jit(solution)/shard_map/ppermute | solution.py:47
  572.0 59.6 %collective-permute-start.26 = (bf16[128,1280]{1,0:T(8,128)(2,1)S(1)}, bf16[128,1280]{1,0:T(8,128)(2,1)S(1)}, u32[]{:S(2)}, u32[]{:S(2)}) collective-permute-start(bf16[128,1280]{1,0:T(8,128)(2,1)S(1)} %get-tuple-element.94), channel_id=1, source_target_pairs={{0,4},{2,6},{4,0},{6,2},{1,5},{3,7},{5,1},{7,3},{8,12},{10,14},{12... | collective-permute-start | bytes 983048 | tf_op jit(solution)/shard_map/ppermute | solution.py:47
  575.4 56.5 %collective-permute-start.54 = (bf16[128,640]{1,0:T(8,128)(2,1)S(1)}, bf16[128,640]{1,0:T(8,128)(2,1)S(1)}, u32[]{:S(2)}, u32[]{:S(2)}) collective-permute-start(bf16[128,640]{1,0:T(8,128)(2,1)S(1)} %get-tuple-element.106), channel_id=1, source_target_pairs={{0,24},{8,16},{16,8},{24,0},{1,25},{9,17},{17,9},{25,1},{2,26},{10... | collective-permute-start | bytes 491528 | tf_op jit(solution)/shard_map/ppermute | solution.py:47
  576.7 55.2 %collective-permute-start.53 = (bf16[128,640]{1,0:T(8,128)(2,1)S(1)}, bf16[128,640]{1,0:T(8,128)(2,1)S(1)}, u32[]{:S(2)}, u32[]{:S(2)}) collective-permute-start(bf16[128,640]{1,0:T(8,128)(2,1)S(1)} %get-tuple-element.107), channel_id=1, source_target_pairs={{0,16},{8,24},{16,0},{24,8},{1,17},{9,25},{17,1},{25,9},{2,18},{10... | collective-permute-start | bytes 491528 | tf_op jit(solution)/shard_map/ppermute | solution.py:47
  603.0 28.9 %collective-permute-start.52 = (bf16[128,640]{1,0:T(8,128)(2,1)S(1)}, bf16[128,640]{1,0:T(8,128)(2,1)S(1)}, u32[]{:S(2)}, u32[]{:S(2)}) collective-permute-start(bf16[128,640]{1,0:T(8,128)(2,1)S(1)} %get-tuple-element.108), channel_id=1, source_target_pairs={{0,8},{8,0},{16,24},{24,16},{1,9},{9,1},{17,25},{25,17},{2,10},{10... | collective-permute-start | bytes 491528 | tf_op jit(solution)/shard_map/ppermute | solution.py:47
  (121 other events, 1200.4 us)
Sparse Core Ops, SparseCore 0:
  10.5 82.4 all-gather.10
  95.5 70.1 all-gather.8
  167.5 58.5 all-gather.12
  377.2 133.6 all-reduce.2
  512.3 119.4 all-gather.18
  633.8 91.1 all-gather.16
  726.6 90.8 all-gather.14
